TPU v7x, 32 devices: a whole 2x2x4 slice. The times are simulated.
32 devices in a mesh: groups: 2 (over x), tile: 16 (over z, y, core).
Axes of the slice: x: 2, y: 2, z: 4, core: 2. Of those that a mesh axis runs over, the one named last changes fastest.
Arguments:
- tracer: float32 [32, 6, 8, 128, 128], P(('groups', 'tile')), parts along dimension 0, may hold values from -6 to 6
- courant_east: bfloat16 [32, 6, 8, 128, 128], P(('groups', 'tile')), parts along dimension 0, may hold values from -1.5 to 1.5
- courant_north: bfloat16 [32, 6, 8, 128, 128], P(('groups', 'tile')), parts along dimension 0, may hold values from -1.5 to 1.5
- diffusivity: bfloat16 [32, 6, 8, 128, 128], P(('groups', 'tile')), parts along dimension 0, may hold values from 0.049804688 to 5
- seam_table: int32 [6, 4, 3], replicated, may hold values from 0 to 5, as said below
Outputs:
- updated: float32 [32, 6, 8, 128, 128], P(('groups', 'tile')), parts along dimension 0
There are 2 independent parts, one for each index of `groups`. A program takes and returns all parts, laid end to end along the dimension named above; an argument that names none is the same for every part. Nothing has to cross between parts.
Inputs may be any that keep to these rules, and one draw needn't show every extreme that they name: seam_table[p, e] = (q, f, r) names the edge f of panel q != p that borders edge e of panel p, and r is 1 where their edge indices run in opposite directions, 0 otherwise; the 24 edges form 12 pairs whose entries name each other with the same r, as on the faces of a cube ; edge 3 of panel 0 borders edge 3 of panel 1.
All inputs are finite; a program needn't handle non-finite values.
Results may differ from a plain program's by a relative error of at most 0.0003.
Values sent between devices are 32-bit elements; how exact they have to be, the bound alone decides.
A program may use at most 128 MiB of HBM per device.

v0:
```python
import math
import jax
import jax.numpy as jnp
from jax import lax
from jax.sharding import PartitionSpec as P

DEPTH = 2


def padded(block, sides, width):
    for axis, dim in sides:
        count = lax.axis_size(axis)
        forward = [(i, i + 1) for i in range(count - 1)]
        forward.append((count - 1, 0))
        backward = [(target, source) for source, target in forward]
        low = lax.ppermute(
            lax.slice_in_dim(block, block.shape[dim] - width, None, axis=dim), axis, forward
        )
        high = lax.ppermute(lax.slice_in_dim(block, 0, width, axis=dim), axis, backward)
        block = jnp.concatenate([low, block, high], axis=dim)
    return block


def from_behind(value, axis, steps):
    count = lax.axis_size(axis)
    pairs = [(source, (source + steps) % count) for source in range(count)]
    return lax.ppermute(value, axis, pairs)


def edge_strips(panels, rows_deep):
    south_rows = jnp.moveaxis(panels[:, :, :, :rows_deep], 3, 1)
    east_rows = jnp.moveaxis(panels[:, :, ::-1, :][:, :, :rows_deep, :], 2, 1)
    north_rows = jnp.moveaxis(panels[:, :, :, ::-1][:, :, :, :rows_deep], 3, 1)
    west_rows = jnp.moveaxis(panels[:, :, :rows_deep, :], 2, 1)
    return jnp.stack([south_rows, east_rows, north_rows, west_rows], axis=1)


def centered(extended, along):
    kept = extended.shape[along] - 4

    def shifted(offset):
        return lax.slice_in_dim(extended, 2 + offset, 2 + offset + kept, axis=along)

    return (8.0 * (shifted(1) - shifted(-1)) - (shifted(2) - shifted(-2))) / 12.0


def advance(panels, ghosts, courant_east, courant_north, diffusivity):
    west_part = jnp.moveaxis(ghosts[:, 3, ::-1], 1, 2)
    east_part = jnp.moveaxis(ghosts[:, 1], 1, 2)
    south_part = jnp.transpose(ghosts[:, 0, ::-1], (0, 2, 3, 1))
    north_part = jnp.transpose(ghosts[:, 2], (0, 2, 3, 1))
    along_first = jnp.concatenate([west_part, panels, east_part], axis=2)
    along_second = jnp.concatenate([south_part, panels, north_part], axis=3)
    forced = panels - (
        courant_east.astype(jnp.float32) * centered(along_first, 2)
        + courant_north.astype(jnp.float32) * centered(along_second, 3)
    )
    coupling = diffusivity.astype(jnp.float32)
    ratios = []
    partial_values = []
    for height in range(panels.shape[1]):
        diagonal = 1.0 + coupling[:, height]
        if height > 0:
            below = coupling[:, height - 1]
            pivot_value = diagonal + below - below * ratios[-1]
            current = (forced[:, height] + below * partial_values[-1]) / pivot_value
        else:
            pivot_value = diagonal
            current = forced[:, height] / pivot_value
        ratios.append(coupling[:, height] / pivot_value)
        partial_values.append(current)
    solved = [partial_values[-1]]
    for height in range(panels.shape[1] - 2, -1, -1):
        solved.insert(0, partial_values[height] + ratios[height] * solved[0])
    return jnp.stack(solved, axis=1)


def panel_tiles(device, across):
    total = across * across
    tile_offset = jnp.arange(6, dtype=jnp.int32) % 2 * (total // 2 + 1)
    return ((device - tile_offset) % total, tile_offset)


def placement(device, across):
    panel_tile, tile_offset = panel_tiles(device, across)
    row_no = panel_tile // across
    col_no = panel_tile % across
    on_edge = jnp.stack(
        [col_no == 0, row_no == across - 1, col_no == across - 1, row_no == 0], axis=1
    ).reshape(24)
    along_edge = jnp.stack([row_no, col_no, row_no, col_no], axis=1).reshape(24)
    return (on_edge, along_edge, panel_tile, tile_offset)


def device_at(edge_no, spot, across):
    return jnp.where(
        edge_no == 0,
        spot * across,
        jnp.where(
            edge_no == 1,
            (across - 1) * across + spot,
            jnp.where(edge_no == 2, spot * across + across - 1, spot),
        ),
    )


def neighbour_step(edge_no, across):
    return jnp.where(
        edge_no == 0, -1, jnp.where(edge_no == 1, across, jnp.where(edge_no == 2, 1, -across))
    )


def sources(seam_table, own_device, across):
    total = across * across
    on_edge, along_edge, panel_tile, tile_offset = placement(own_device, across)
    flat_table = seam_table.reshape(24, 3)
    ghost_edge = jnp.arange(24, dtype=jnp.int32) % 4
    ghost_panel = jnp.arange(24, dtype=jnp.int32) // 4
    turned_spot = jnp.where(flat_table[:, 2] == 1, across - 1 - along_edge, along_edge)
    far_tile = device_at(flat_table[:, 1], turned_spot, across)
    far_device = (far_tile + jnp.take(tile_offset, flat_table[:, 0])) % total
    near_device = (own_device + neighbour_step(ghost_edge, across)) % total
    source_device = jnp.where(on_edge, far_device, near_device)
    source_block = jnp.where(
        on_edge, flat_table[:, 0] * 4 + flat_table[:, 1], ghost_panel * 4 + (ghost_edge + 2) % 4
    )
    reverse_it = jnp.logical_and(on_edge, flat_table[:, 2] == 1)
    return (on_edge, flat_table, source_device, source_block, reverse_it, panel_tile)


def shards(tracer, courant_east, courant_north, diffusivity, seam_table):
    panels = tracer[0]
    tile_count = lax.axis_size("tile")
    across = math.isqrt(tile_count)
    own_device = lax.axis_index("tile")
    strips = edge_strips(panels, DEPTH)
    blocks = strips.reshape((24,) + strips.shape[2:])
    on_edge, flat_table, source_device, source_block, reverse_it, panel_tile = sources(
        seam_table, own_device, across
    )
    row_no = panel_tile // across
    col_no = panel_tile % across
    side_first = jnp.where(col_no == across - 1, 2, 0).astype(jnp.int32)
    side_second = jnp.where(row_no == 0, 3, 1).astype(jnp.int32)
    first_rows = jnp.take_along_axis(strips, side_first[:, None, None, None, None], axis=1)[:, 0]
    second_rows = jnp.take_along_axis(strips, side_second[:, None, None, None, None], axis=1)[:, 0]
    packed = jnp.concatenate([first_rows, second_rows], axis=0)
    collected = lax.all_gather(packed[None], "tile", axis=0, tiled=True)
    slot_in = jnp.where(flat_table[:, 1] % 2 == 0, 0, 6) + flat_table[:, 0]
    picked = jnp.take(
        collected.reshape((tile_count * 12,) + blocks.shape[1:]),
        source_device * 12 + slot_in,
        axis=0,
        mode="clip",
    )
    picked = jnp.where(reverse_it[:, None, None, None], picked[..., ::-1], picked)
    both_rows = jnp.stack([strips[:, 0], strips[:, 2]], axis=0)
    widened = padded(both_rows, (("tile", 0),), 1)
    from_west = from_behind(strips[:, 1], "tile", across)
    from_east = from_behind(strips[:, 3], "tile", -across)
    inside = jnp.stack([widened[0], from_east, widened[3], from_west], axis=1).reshape(blocks.shape)
    ghosts = jnp.where(on_edge[:, None, None, None], picked, inside)
    updated = advance(
        panels, ghosts.reshape(strips.shape), courant_east[0], courant_north[0], diffusivity[0]
    )
    return updated[None]


def solution(mesh):
    placed = (
        P(("groups", "tile"), None, None, None, None),
        P(("groups", "tile"), None, None, None, None),
        P(("groups", "tile"), None, None, None, None),
        P(("groups", "tile"), None, None, None, None),
        P(),
    )
    return jax.shard_map(
        shards,
        mesh=mesh,
        in_specs=placed,
        out_specs=P(("groups", "tile"), None, None, None, None),
        check_vma=False,
    )
```

profile of v0, /device:TPU:0, one launch (start us, length us, event | category | flops | bytes accessed | tf_op | source)
XLA Modules:
  0.0 114.8 jit_solution(10395726204144280213)
XLA Ops:
  6.5 0.0 all-gather.3.cloned.1.call-start
  6.6 1.1 slice_bitcast_fusion
  7.7 5.5 %fusion.60 = (f32[6,8,128,2]{3,2,1,0:T(8,128)}, f32[6,8,128,2]{3,2,1,0:T(8,128)S(1)}) fusion(f32[6,8,128,128]{3,2,1,0:T(8,128)} %bitcast.97), kind=kLoop, calls=%fused_computation.177 | loop fusion | bytes 196608 | tf_op jit(solution)/shard_map/slice | solution.py:33
  13.2 0.1 slice.139
  13.3 2.4 %copy.55 = f32[6,8,128,2]{2,3,1,0:T(2,128)S(1)} copy(f32[6,8,128,2]{3,2,1,0:T(8,128)} %get-tuple-element.24) | data formatting | bytes 98304
  15.7 0.1 slice.141
  15.8 1.2 %copy.54 = f32[6,8,128,2]{2,3,1,0:T(2,128)S(1)} copy(f32[6,8,128,2]{3,2,1,0:T(8,128)S(1)} %get-tuple-element.25) | data formatting | bytes 98304
  17.0 0.1 pad_maximum_fusion.4
  17.1 0.6 gather_fusion.3
  17.7 0.6 gather_fusion.2
  18.4 0.1 fusion.28
  18.4 0.1 fusion.27
  18.6 0.7 copy.44
  19.2 0.0 all-gather.3.cloned.1.call-update
  19.3 3.1 %collective-permute-start.3 = (f32[6,2,8,128]{3,1,2,0:T(2,128)S(1)}, f32[6,2,8,128]{3,1,2,0:T(2,128)S(1)}, u32[]{:S(2)}, u32[]{:S(2)}) collective-permute-start(f32[6,2,8,128]{3,1,2,0:T(2,128)S(1)} %bitcast.107), channel_id=1, source_target_pairs={{0,4},{1,5},{2,6},{3,7},{4,8},{5,9},{6,10},{7,11},{8,12},{9,13},{1... | collective-permute-start | bytes 147464 | tf_op jit(solution)/shard_map/ppermute | solution.py:27
  22.4 2.1 %collective-permute-start.1 = (f32[6,2,8,128]{3,1,2,0:T(2,128)S(1)}, f32[6,2,8,128]{3,1,2,0:T(2,128)S(1)}, u32[]{:S(2)}, u32[]{:S(2)}) collective-permute-start(f32[6,2,8,128]{3,1,2,0:T(2,128)S(1)} %get-tuple-element.22), channel_id=1, source_target_pairs={{0,12},{1,13},{2,14},{3,15},{4,0},{5,1},{6,2},{7,3},{8,4},{9,5},{1... | collective-permute-start | bytes 147464 | tf_op jit(solution)/shard_map/ppermute | solution.py:27
  24.5 0.0 collective-permute-start
  24.5 4.4 %collective-permute-start.2 = (f32[1,6,2,8,128]{4,3,2,1,0:T(8,128)S(1)}, f32[1,6,2,8,128]{4,3,2,1,0:T(8,128)S(1)}, u32[]{:S(2)}, u32[]{:S(2)}) collective-permute-start(f32[1,6,2,8,128]{4,3,2,1,0:T(8,128)S(1)} %copy.47), channel_id=1, source_target_pairs={{1,0},{2,1},{3,2},{4,3},{5,4},{6,5},{7,6},{8,7},{9,8},{10,9},{11,1... | collective-permute-start | bytes 147464 | tf_op jit(solution)/shard_map/ppermute | solution.py:19
  29.0 0.1 pad_add_fusion.1
  29.1 0.1 broadcast_in_dim.51
  29.1 0.1 reshape.440
  29.3 0.1 pad_add_fusion
  29.3 0.1 reshape.441
  29.4 0.1 copy.41
  29.5 0.1 reshape.438
  29.6 0.7 gather_fusion
  30.4 2.0 %bitcast_convert_fusion = f32[6,8,128,128]{3,2,1,0:T(8,128)} fusion(bf16[1,6,8,128,128]{4,3,2,1,0:T(8,128)(2,1)S(1)} %copy-done.2), kind=kLoop, calls=%fused_computation.34 | loop fusion | flops 786432 | bytes 4718592 | tf_op jit(solution)/shard_map/convert_element_type | solution.py:58
  32.4 0.0 collective-permute-done
  32.5 0.0 collective-permute-done.2
  32.5 0.0 collective-permute-done.3
  32.5 0.0 collective-permute-done.1
  32.5 0.1 pad_maximum_fusion.5
  32.7 29.1 %all-gather.3.cloned.1.call-done = f32[192,2,8,128]{3,2,1,0:T(8,128)} async-done(((f32[12,2,8,128]{3,2,1,0:T(8,128)}), f32[192,2,8,128]{3,2,1,0:T(8,128)}) %all-gather.3.cloned.1.call-update) | async-done | bytes 1572880 | tf_op jit(solution)/shard_map/all_gather | solution.py:148
  61.8 2.0 %gather_fusion.1 = f32[24,2,8,128]{3,2,1,0:T(8,128)S(1)} fusion(f32[192,2,8,128]{3,2,1,0:T(8,128)} %all-gather.3.cloned.1.call-done, s32[1024]{0:T(1024)S(1)} %pad_clamp_fusion), kind=kCustom, calls=%fused_computation.3 | custom fusion | bytes 393312 | tf_op jit(solution)/shard_map/jit(_take)/gather | solution.py:150
  63.7 0.1 rev.11
  63.8 0.1 bitcast_select_fusion
  64.0 0.1 rev.12
  64.2 2.2 %copy.58 = f32[6,1,2,8,128]{2,4,3,0,1:T(8,128)} copy(f32[6,1,2,8,128]{4,3,2,1,0:T(8,128)S(1)} %get-tuple-element.26) | data formatting | bytes 98304
  66.4 2.3 %copy.59 = f32[6,1,2,8,128]{2,4,3,0,1:T(8,128)} copy(f32[6,1,2,8,128]{4,3,2,1,0:T(8,128)S(1)} %get-tuple-element.29) | data formatting | bytes 98304
  68.7 26.0 %rev.13 = f32[6,1,2,8,128]{2,4,3,0,1:T(8,128)} reverse(f32[6,1,2,8,128]{2,4,3,0,1:T(8,128)} %copy.59), dimensions={2} | reverse | bytes 98304 | tf_op jit(solution)/shard_map/rev | solution.py:50
  94.6 9.8 %fusion.7 = f32[6,8,128,128]{3,2,1,0:T(8,128)S(1)} fusion(f32[6,8,128,128]{3,2,1,0:T(8,128)S(1)} %bitcast.98, f32[6,8,2,128]{3,2,1,0:T(2,128)S(1)} %bitcast.110, f32[6,8,2,128]{3,2,1,0:T(2,128)S(1)} %bitcast.111, f32[6,8,128,2]{3,2,1,0:T(8,128)} %bitcast.100, f32[6,8,128,2]{3,2,1,0:T(8,128)} %bitcast.99, bf16[1,6,8,128,128]{4,3,2,1,0:T(8,128)(2,1)} %param.9, ...), kind=kLoop, calls=%fused_computation.19 | loop fusion | flops 18874368 | bytes 9633792 | tf_op jit(solution)/shard_map/sub | solution.py:54
  104.5 0.7 fusion.22
  105.2 0.7 add_dynamic-update-slice_fusion
  105.9 0.1 constant_dynamic-update-slice_fusion.5
  106.0 0.1 constant_dynamic-update-slice_fusion.3
  106.1 0.1 constant_dynamic-update-slice_fusion.1
  106.2 0.0 copy-start.3
  106.3 1.7 %copy-done.3 = f32[6,8,128,128]{3,2,1,0:T(8,128)} copy-done((f32[6,8,128,128]{3,2,1,0:T(8,128)}, f32[6,8,128,128]{3,2,1,0:T(8,128)S(1)}, u32[]{:S(2)}) %copy-start.3) | copy-done | bytes 3145752
  (36 shorter events, 0.5 us)
Async XLA Ops:
  6.5 55.2 %all-gather.3.cloned.1.call-start = ((), (), s32[]{:S(2)}) async-start(), calls=%async_computation | async-start | bytes 1671168 | tf_op jit(solution)/shard_map/all_gather | solution.py:148
  15.7 13.8 %copy-start.4 = (s32[6,4,3]{0,1,2:T(4,128)S(1)}, s32[6,4,3]{0,1,2:T(4,128)}, u32[]{:S(2)}) copy-start(s32[6,4,3]{0,1,2:T(4,128)} %param.11) | copy-start | bytes 868
  17.0 13.4 %copy-start.2 = (bf16[1,6,8,128,128]{4,3,2,1,0:T(8,128)(2,1)S(1)}, bf16[1,6,8,128,128]{4,3,2,1,0:T(8,128)(2,1)}, u32[]{:S(2)}) copy-start(bf16[1,6,8,128,128]{4,3,2,1,0:T(8,128)(2,1)} %param.10) | copy-start | bytes 4718596
  19.3 13.2 %collective-permute-start.3 = (f32[6,2,8,128]{3,1,2,0:T(2,128)S(1)}, f32[6,2,8,128]{3,1,2,0:T(2,128)S(1)}, u32[]{:S(2)}, u32[]{:S(2)}) collective-permute-start(f32[6,2,8,128]{3,1,2,0:T(2,128)S(1)} %bitcast.107), channel_id=1, source_target_pairs={{0,4},{1,5},{2,6},{3,7},{4,8},{5,9},{6,10},{7,11},{8,12},{9,13},{1... | collective-permute-start | bytes 147464 | tf_op jit(solution)/shard_map/ppermute | solution.py:27
  22.4 10.1 %collective-permute-start.1 = (f32[6,2,8,128]{3,1,2,0:T(2,128)S(1)}, f32[6,2,8,128]{3,1,2,0:T(2,128)S(1)}, u32[]{:S(2)}, u32[]{:S(2)}) collective-permute-start(f32[6,2,8,128]{3,1,2,0:T(2,128)S(1)} %get-tuple-element.22), channel_id=1, source_target_pairs={{0,12},{1,13},{2,14},{3,15},{4,0},{5,1},{6,2},{7,3},{8,4},{9,5},{1... | collective-permute-start | bytes 147464 | tf_op jit(solution)/shard_map/ppermute | solution.py:27
  24.5 8.0 %collective-permute-start = (f32[1,6,2,8,128]{4,3,2,1,0:T(8,128)S(1)}, f32[1,6,2,8,128]{4,3,2,1,0:T(8,128)S(1)}, u32[]{:S(2)}, u32[]{:S(2)}) collective-permute-start(f32[1,6,2,8,128]{4,3,2,1,0:T(8,128)S(1)} %copy.45), channel_id=1, source_target_pairs={{0,1},{1,2},{2,3},{3,4},{4,5},{5,6},{6,7},{7,8},{8,9},{9,10},{10,1... | collective-permute-start | bytes 147464 | tf_op jit(solution)/shard_map/ppermute | solution.py:16
  24.5 8.0 %collective-permute-start.2 = (f32[1,6,2,8,128]{4,3,2,1,0:T(8,128)S(1)}, f32[1,6,2,8,128]{4,3,2,1,0:T(8,128)S(1)}, u32[]{:S(2)}, u32[]{:S(2)}) collective-permute-start(f32[1,6,2,8,128]{4,3,2,1,0:T(8,128)S(1)} %copy.47), channel_id=1, source_target_pairs={{1,0},{2,1},{3,2},{4,3},{5,4},{6,5},{7,6},{8,7},{9,8},{10,9},{11,1... | collective-permute-start | bytes 147464 | tf_op jit(solution)/shard_map/ppermute | solution.py:19
  68.7 26.0 %copy-start = (f32[1,6,8,128,128]{4,3,2,1,0:T(8,128)S(1)}, f32[1,6,8,128,128]{4,3,2,1,0:T(8,128)}, u32[]{:S(2)}) copy-start(f32[1,6,8,128,128]{4,3,2,1,0:T(8,128)} %param.7) | copy-start | bytes 9437188
  94.6 9.9 %copy-start.1 = (f32[6,8,128,128]{3,2,1,0:T(8,128)S(1)}, f32[6,8,128,128]{3,2,1,0:T(8,128)}, u32[]{:S(2)}) copy-start(f32[6,8,128,128]{3,2,1,0:T(8,128)} %bitcast_convert_fusion) | copy-start | bytes 9437188
  106.2 1.7 %copy-start.3 = (f32[6,8,128,128]{3,2,1,0:T(8,128)}, f32[6,8,128,128]{3,2,1,0:T(8,128)S(1)}, u32[]{:S(2)}) copy-start(f32[6,8,128,128]{3,2,1,0:T(8,128)S(1)} %constant_dynamic-update-slice_fusion) | copy-start | bytes 9437188
Sparse Core Ops, SparseCore 0:
  19.4 42.3 all-gather.2
where the time goes:
time: 117 us; the launch traced here: 115 us
  local copies, waits for them, and re-layouts  48 us (41%)
  waiting for transfers between devices  29.1 us (25%)
  other arithmetic  14.3 us (12%)
  between operations  13.7 us (12%)
  starting transfers between devices  9.64 us (8%)
    all_gather x1, waiting for transfers between devices, shards(): collected = lax.all_gather(packed[None], 'tile', axis=0, tiled=True)  29.1 us
    rev x1, local copies, waits for them, and re-layouts, advance(): south_part = jnp.transpose(ghosts[:, 0, ::-1], (0, 2, 3, 1))  26 us
    unnamed x20, local copies, waits for them, and re-layouts  9.93 us
    sub x1, other arithmetic, advance(): panels - (courant_east.astype(jnp.float32) * centered(along_first, 2) + c...  9.84 us
    slice x2, local copies, waits for them, and re-layouts, edge_strips(): north_rows = jnp.moveaxis(panels[:, :, :, ::-1][:, :, :, :rows_deep], 3, 1)  5.6 us
    ppermute x2, starting transfers between devices, from_behind(): return lax.ppermute(value, axis, pairs)  5.2 us
    ppermute x1, starting transfers between devices, padded(): lax.ppermute(lax.slice_in_dim(block, 0, width, axis=dim), axis, backward)  4.44 us
  transfers between devices with their start and end apart: 5, of which 1 were waited for; matrix products, arithmetic and copies ran while one was open for 3% of the time, Pallas kernels for 0%

commit v1 on v0

--- a/solution.py
+++ b/solution.py
@@ -145,7 +145,9 @@
     first_rows = jnp.take_along_axis(strips, side_first[:, None, None, None, None], axis=1)[:, 0]
     second_rows = jnp.take_along_axis(strips, side_second[:, None, None, None, None], axis=1)[:, 0]
     packed = jnp.concatenate([first_rows, second_rows], axis=0)
-    collected = lax.all_gather(packed[None], "tile", axis=0, tiled=True)
+    collected = jnp.concatenate(
+        lax.all_to_all(jnp.stack([packed[None]] * lax.axis_size("tile")), "tile", 0, 0), axis=0
+    )
     slot_in = jnp.where(flat_table[:, 1] % 2 == 0, 0, 6) + flat_table[:, 0]
     picked = jnp.take(
         collected.reshape((tile_count * 12,) + blocks.shape[1:]),

time: 117 us -> 105 us (0.90)
  the two profiles are of different devices: /device:TPU:0 before, /device:TPU:12 now
where the time goes in v1:
time: 105 us; the launch traced here: 103 us
  local copies, waits for them, and re-layouts  50 us (48%)
  waiting for transfers between devices  26.7 us (25%)
  other arithmetic  16.4 us (16%)
  starting transfers between devices  10 us (10%)
    ppermute x2, waiting for transfers between devices, from_behind(): return lax.ppermute(value, axis, pairs)  26.7 us
    rev x1, local copies, waits for them, and re-layouts, advance(): south_part = jnp.transpose(ghosts[:, 0, ::-1], (0, 2, 3, 1))  25.9 us
    unnamed x20, local copies, waits for them, and re-layouts  10.6 us
    sub x1, other arithmetic, advance(): panels - (courant_east.astype(jnp.float32) * centered(along_first, 2) + c...  9.74 us
    all_to_all x1, starting transfers between devices, shards(): lax.all_to_all(jnp.stack([packed[None]] * lax.axis_size('tile')), 'tile',...  6.24 us
    slice x2, local copies, waits for them, and re-layouts, edge_strips(): north_rows = jnp.moveaxis(panels[:, :, :, ::-1][:, :, :, :rows_deep], 3, 1)  5.6 us
  transfers between devices with their start and end apart: 5, of which 2 were waited for; matrix products, arithmetic and copies ran while one was open for 8% of the time, Pallas kernels for 0%

profile of v1, /device:TPU:12, one launch (start us, length us, event | category | flops | bytes accessed | tf_op | source)
XLA Modules:
  0.0 103.4 jit_solution(2417855888968502306)
XLA Ops:
  0.1 1.1 %slice_bitcast_fusion = (f32[6,1,2,8,128]{4,2,3,0,1:T(2,128)S(1)}, f32[6,2,8,128]{3,1,2,0:T(2,128)S(1)}, f32[6,8,2,128]{3,2,1,0:T(2,128)S(1)}) fusion(f32[6,8,128,128]{3,2,1,0:T(8,128)} %bitcast.97), kind=kLoop, calls=%fused_computation.84 | loop fusion | bytes 245760 | tf_op jit(solution)/shard_map/stack | solution.py:35
  1.1 5.5 %fusion.60 = (f32[6,8,128,2]{3,2,1,0:T(8,128)}, f32[6,8,128,2]{3,2,1,0:T(8,128)S(1)}) fusion(f32[6,8,128,128]{3,2,1,0:T(8,128)} %bitcast.98), kind=kLoop, calls=%fused_computation.177 | loop fusion | bytes 196608 | tf_op jit(solution)/shard_map/slice | solution.py:33
  6.6 0.1 slice.139
  6.8 2.4 %copy.56 = f32[6,8,128,2]{2,3,1,0:T(2,128)S(1)} copy(f32[6,8,128,2]{3,2,1,0:T(8,128)} %get-tuple-element.24) | data formatting | bytes 98304
  9.1 0.1 slice.141
  9.3 1.2 %copy.55 = f32[6,8,128,2]{2,3,1,0:T(2,128)S(1)} copy(f32[6,8,128,2]{3,2,1,0:T(8,128)S(1)} %get-tuple-element.25) | data formatting | bytes 98304
  10.4 0.1 pad_maximum_fusion.4
  10.6 0.6 gather_fusion.3
  11.2 0.0 copy-start.2
  11.2 0.6 gather_fusion.2
  11.8 0.1 fusion.28
  11.9 0.1 fusion.27
  12.1 1.3 %stack.58 = f32[16,1,12,2,8,128]{5,4,3,2,1,0:T(8,128)} broadcast(f32[12,2,8,128]{3,2,1,0:T(8,128)S(1)} %copy.45), dimensions={2,3,4,5} | broadcast | bytes 1671168 | tf_op jit(solution)/shard_map/stack | solution.py:149
  13.4 6.2 %all-to-all-start = ((f32[16,1,12,2,8,128]{5,4,3,2,1,0:T(8,128)}), f32[16,1,12,2,8,128]{5,4,3,2,1,0:T(8,128)S(1)}, u32[]{:S(2)}, u32[]{:S(2)}) async-start(f32[16,1,12,2,8,128]{5,4,3,2,1,0:T(8,128)} %stack.58), calls=%async_computation | async-start | bytes 3145728 | tf_op jit(solution)/shard_map/all_to_all | solution.py:149
  19.6 1.5 %collective-permute-start.3 = (f32[6,2,8,128]{3,1,2,0:T(2,128)S(1)}, f32[6,2,8,128]{3,1,2,0:T(2,128)S(1)}, u32[]{:S(2)}, u32[]{:S(2)}) collective-permute-start(f32[6,2,8,128]{3,1,2,0:T(2,128)S(1)} %bitcast.109), channel_id=1, source_target_pairs={{0,4},{1,5},{2,6},{3,7},{4,8},{5,9},{6,10},{7,11},{8,12},{9,13},{1... | collective-permute-start | bytes 147464 | tf_op jit(solution)/shard_map/ppermute | solution.py:27
  21.1 0.6 collective-permute-start.1
  21.7 1.7 %collective-permute-start.2 = (f32[1,6,2,8,128]{4,3,2,1,0:T(8,128)S(1)}, f32[1,6,2,8,128]{4,3,2,1,0:T(8,128)S(1)}, u32[]{:S(2)}, u32[]{:S(2)}) collective-permute-start(f32[1,6,2,8,128]{4,3,2,1,0:T(8,128)S(1)} %copy.48), channel_id=1, source_target_pairs={{1,0},{2,1},{3,2},{4,3},{5,4},{6,5},{7,6},{8,7},{9,8},{10,9},{11,1... | collective-permute-start | bytes 147464 | tf_op jit(solution)/shard_map/ppermute | solution.py:19
  23.5 0.1 pad_add_fusion.1
  23.6 0.6 broadcast_in_dim.48
  24.2 0.7 reshape.438
  24.9 0.1 pad_add_fusion
  24.9 0.6 reshape.439
  25.6 0.8 copy.42
  26.3 0.7 reshape.437
  27.0 0.7 fusion.54
  27.7 0.7 gather_fusion
  28.4 0.7 bitcast_and_fusion
  29.1 0.8 fusion.51
  29.9 2.0 %bitcast_convert_fusion = f32[6,8,128,128]{3,2,1,0:T(8,128)} fusion(bf16[1,6,8,128,128]{4,3,2,1,0:T(8,128)(2,1)S(1)} %copy-done.2), kind=kLoop, calls=%fused_computation.34 | loop fusion | flops 786432 | bytes 4718592 | tf_op jit(solution)/shard_map/convert_element_type | solution.py:58
  32.0 0.0 collective-permute-done.2
  32.1 24.7 %collective-permute-done.3 = f32[6,2,8,128]{3,1,2,0:T(2,128)S(1)} collective-permute-done((f32[6,2,8,128]{3,1,2,0:T(2,128)S(1)}, f32[6,2,8,128]{3,1,2,0:T(2,128)S(1)}, u32[]{:S(2)}, u32[]{:S(2)}) %collective-permute-start.3) | collective-permute-done | bytes 49184 | tf_op jit(solution)/shard_map/ppermute | solution.py:27
  56.8 2.0 %collective-permute-done.1 = f32[6,2,8,128]{3,1,2,0:T(2,128)S(1)} collective-permute-done((f32[6,2,8,128]{3,1,2,0:T(2,128)S(1)}, f32[6,2,8,128]{3,1,2,0:T(2,128)S(1)}, u32[]{:S(2)}, u32[]{:S(2)}) %collective-permute-start.1) | collective-permute-done | bytes 49184 | tf_op jit(solution)/shard_map/ppermute | solution.py:27
  58.8 0.1 pad_maximum_fusion.5
  58.9 0.6 gather_fusion.1
  59.5 0.1 rev.11
  59.6 0.1 bitcast_select_fusion
  59.8 0.1 rev.12
  59.9 2.2 %copy.59 = f32[6,1,2,8,128]{2,4,3,0,1:T(8,128)} copy(f32[6,1,2,8,128]{4,3,2,1,0:T(8,128)S(1)} %get-tuple-element.26) | data formatting | bytes 98304
  62.1 2.3 %copy.60 = f32[6,1,2,8,128]{2,4,3,0,1:T(8,128)} copy(f32[6,1,2,8,128]{4,3,2,1,0:T(8,128)S(1)} %get-tuple-element.29) | data formatting | bytes 98304
  64.4 25.9 %rev.13 = f32[6,1,2,8,128]{2,4,3,0,1:T(8,128)} reverse(f32[6,1,2,8,128]{2,4,3,0,1:T(8,128)} %copy.60), dimensions={2} | reverse | bytes 98304 | tf_op jit(solution)/shard_map/rev | solution.py:50
  90.3 9.7 %fusion.7 = f32[6,8,128,128]{3,2,1,0:T(8,128)S(1)} fusion(f32[6,8,128,128]{3,2,1,0:T(8,128)S(1)} %bitcast.99, f32[6,8,2,128]{3,2,1,0:T(2,128)S(1)} %bitcast.112, f32[6,8,2,128]{3,2,1,0:T(2,128)S(1)} %bitcast.113, f32[6,8,128,2]{3,2,1,0:T(8,128)} %bitcast.101, f32[6,8,128,2]{3,2,1,0:T(8,128)} %bitcast.100, bf16[1,6,8,128,128]{4,3,2,1,0:T(8,128)(2,1)} %param.9, ...), kind=kLoop, calls=%fused_computation.19 | loop fusion | flops 18874368 | bytes 9633792 | tf_op jit(solution)/shard_map/sub | solution.py:54
  100.0 0.7 fusion.22
  100.7 0.7 add_dynamic-update-slice_fusion
  101.5 0.1 constant_dynamic-update-slice_fusion.5
  101.6 0.1 constant_dynamic-update-slice_fusion.3
  101.7 0.1 constant_dynamic-update-slice_fusion.1
  101.8 0.0 copy-start.3
  101.8 1.7 %copy-done.3 = f32[6,8,128,128]{3,2,1,0:T(8,128)} copy-done((f32[6,8,128,128]{3,2,1,0:T(8,128)}, f32[6,8,128,128]{3,2,1,0:T(8,128)S(1)}, u32[]{:S(2)}) %copy-start.3) | copy-done | bytes 3145752
  (36 shorter events, 0.5 us)
Async XLA Ops:
  11.2 18.7 %copy-start.2 = (bf16[1,6,8,128,128]{4,3,2,1,0:T(8,128)(2,1)S(1)}, bf16[1,6,8,128,128]{4,3,2,1,0:T(8,128)(2,1)}, u32[]{:S(2)}) copy-start(bf16[1,6,8,128,128]{4,3,2,1,0:T(8,128)(2,1)} %param.10) | copy-start | bytes 4718596
  13.4 45.5 %all-to-all-start = ((f32[16,1,12,2,8,128]{5,4,3,2,1,0:T(8,128)}), f32[16,1,12,2,8,128]{5,4,3,2,1,0:T(8,128)S(1)}, u32[]{:S(2)}, u32[]{:S(2)}) async-start(f32[16,1,12,2,8,128]{5,4,3,2,1,0:T(8,128)} %stack.58), calls=%async_computation | async-start | bytes 3145728 | tf_op jit(solution)/shard_map/all_to_all | solution.py:149
  19.6 37.1 %collective-permute-start.3 = (f32[6,2,8,128]{3,1,2,0:T(2,128)S(1)}, f32[6,2,8,128]{3,1,2,0:T(2,128)S(1)}, u32[]{:S(2)}, u32[]{:S(2)}) collective-permute-start(f32[6,2,8,128]{3,1,2,0:T(2,128)S(1)} %bitcast.109), channel_id=1, source_target_pairs={{0,4},{1,5},{2,6},{3,7},{4,8},{5,9},{6,10},{7,11},{8,12},{9,13},{1... | collective-permute-start | bytes 147464 | tf_op jit(solution)/shard_map/ppermute | solution.py:27
  21.1 37.6 %collective-permute-start.1 = (f32[6,2,8,128]{3,1,2,0:T(2,128)S(1)}, f32[6,2,8,128]{3,1,2,0:T(2,128)S(1)}, u32[]{:S(2)}, u32[]{:S(2)}) collective-permute-start(f32[6,2,8,128]{3,1,2,0:T(2,128)S(1)} %get-tuple-element.22), channel_id=1, source_target_pairs={{0,12},{1,13},{2,14},{3,15},{4,0},{5,1},{6,2},{7,3},{8,4},{9,5},{1... | collective-permute-start | bytes 147464 | tf_op jit(solution)/shard_map/ppermute | solution.py:27
  21.7 10.3 %collective-permute-start = (f32[1,6,2,8,128]{4,3,2,1,0:T(8,128)S(1)}, f32[1,6,2,8,128]{4,3,2,1,0:T(8,128)S(1)}, u32[]{:S(2)}, u32[]{:S(2)}) collective-permute-start(f32[1,6,2,8,128]{4,3,2,1,0:T(8,128)S(1)} %copy.46), channel_id=1, source_target_pairs={{0,1},{1,2},{2,3},{3,4},{4,5},{5,6},{6,7},{7,8},{8,9},{9,10},{10,1... | collective-permute-start | bytes 147464 | tf_op jit(solution)/shard_map/ppermute | solution.py:16
  21.7 10.3 %collective-permute-start.2 = (f32[1,6,2,8,128]{4,3,2,1,0:T(8,128)S(1)}, f32[1,6,2,8,128]{4,3,2,1,0:T(8,128)S(1)}, u32[]{:S(2)}, u32[]{:S(2)}) collective-permute-start(f32[1,6,2,8,128]{4,3,2,1,0:T(8,128)S(1)} %copy.48), channel_id=1, source_target_pairs={{1,0},{2,1},{3,2},{4,3},{5,4},{6,5},{7,6},{8,7},{9,8},{10,9},{11,1... | collective-permute-start | bytes 147464 | tf_op jit(solution)/shard_map/ppermute | solution.py:19
  29.9 29.7 %copy-start.4 = (pred[24]{0:T(512)(128)(4,1)S(1)}, pred[24]{0:T(512)(128)(4,1)}, u32[]{:S(2)}) copy-start(pred[24]{0:T(512)(128)(4,1)} %broadcast_in_dim.48) | copy-start | bytes 76
  64.4 25.9 %copy-start = (f32[1,6,8,128,128]{4,3,2,1,0:T(8,128)S(1)}, f32[1,6,8,128,128]{4,3,2,1,0:T(8,128)}, u32[]{:S(2)}) copy-start(f32[1,6,8,128,128]{4,3,2,1,0:T(8,128)} %param.7) | copy-start | bytes 9437188
  90.3 9.8 %copy-start.1 = (f32[6,8,128,128]{3,2,1,0:T(8,128)S(1)}, f32[6,8,128,128]{3,2,1,0:T(8,128)}, u32[]{:S(2)}) copy-start(f32[6,8,128,128]{3,2,1,0:T(8,128)} %bitcast_convert_fusion) | copy-start | bytes 9437188
  101.8 1.7 %copy-start.3 = (f32[6,8,128,128]{3,2,1,0:T(8,128)}, f32[6,8,128,128]{3,2,1,0:T(8,128)S(1)}, u32[]{:S(2)}) copy-start(f32[6,8,128,128]{3,2,1,0:T(8,128)S(1)} %constant_dynamic-update-slice_fusion) | copy-start | bytes 9437188
